TPU v7x, 32 devices: a whole 2x2x4 slice. The times are simulated.
32 devices in a mesh: prow: 8 (over z, x), pcol: 4 (over y, core).
Axes of the slice: x: 2, y: 2, z: 4, core: 2. Of those that a mesh axis runs over, the one named last changes fastest.
Arguments:
- cross_cov: float32 [4, 8, 256, 8, 4, 256], P(None, 'prow', None, None, 'pcol'), may hold values from -6 to 6
- left_factor: float32 [4, 8, 256, 512], P(None, 'prow', None, 'pcol'), may hold values from -1 to 3, as said below
- right_factor: float32 [8, 4, 256, 512], P(None, 'pcol', None, 'prow'), may hold values from -1 to 3, as said below
Outputs:
- whitened: float32 [4, 8, 256, 8, 4, 256], P(None, 'prow', None, None, 'pcol')
Inputs may be any that keep to these rules, and one draw needn't show every extreme that they name: `left_factor`: the diagonal entries of the diagonal blocks lie between 1.5 and 2. `right_factor`: the diagonal entries of the diagonal blocks lie between 1.5 and 2.
All inputs are finite; a program needn't handle non-finite values.
Results may differ from a plain program's by a relative error of at most 0.0001.
Values sent between devices are 32-bit elements; how exact they have to be, the bound alone decides.
A program may use at most 128 MiB of HBM per device.

v0:
```python
import jax
import jax.numpy as jnp
from jax import lax
from jax.sharding import PartitionSpec as P

STEPS = 2


def spread(x, axis, root):
    mine = lax.axis_index(axis) == root
    return lax.psum(jnp.where(mine, x, jnp.zeros_like(x)), axis)


def solve_left(operands):
    diag_block, owned_rows = operands
    return jax.scipy.linalg.solve_triangular(diag_block, owned_rows, lower=True)


def solve_right(operands):
    diag_block, owned_cols = operands
    return jax.scipy.linalg.solve_triangular(diag_block, owned_cols.T, lower=True).T


def nothing_left(operands):
    return jnp.zeros_like(operands[1])


def shards(cross_cov, left_factor, right_factor):
    rows_axis = lax.axis_size("prow")
    cols_axis = lax.axis_size("pcol")
    my_row = lax.axis_index("prow")
    my_col = lax.axis_index("pcol")
    row_blocks = cross_cov.shape[0]
    block_size = cross_cov.shape[2]
    col_blocks = cross_cov.shape[3]
    left_rows = lax.all_gather(left_factor, "pcol", axis=3, tiled=True)[:, 0]
    right_rows = lax.all_gather(right_factor, "prow", axis=3, tiled=True)[:, 0]
    matrix = cross_cov.reshape(row_blocks, block_size, col_blocks * block_size)
    row_index = (jnp.arange(row_blocks) * rows_axis + my_row).reshape(row_blocks, 1, 1)

    def left_update(current, solved, block_step):
        first_col = block_step * block_size
        factor = left_rows[:, :, first_col : first_col + block_size]
        update = jnp.einsum("cij,jn->cin", factor, solved, precision=lax.Precision.HIGHEST)
        return jnp.where(
            row_index > block_step,
            current - update,
            jnp.where(row_index == block_step, solved[None], current),
        )

    for block_step in range(STEPS):
        local_block = block_step // rows_axis
        first_col = block_step * block_size
        diag_block = left_rows[local_block, :, first_col : first_col + block_size]
        solved = lax.cond(
            my_row == block_step % rows_axis,
            solve_left,
            nothing_left,
            (diag_block, matrix[local_block]),
        )
        solved = spread(solved, "prow", block_step % rows_axis)
        matrix = left_update(matrix, solved, block_step)
    columns = matrix.reshape(row_blocks * block_size, col_blocks, block_size)
    col_index = (jnp.arange(col_blocks) * cols_axis + my_col).reshape(1, col_blocks, 1)

    def right_update(current, solved, block_step):
        first_col = block_step * block_size
        factor = right_rows[:, :, first_col : first_col + block_size]
        update = jnp.einsum("rj,dsj->rds", solved, factor, precision=lax.Precision.HIGHEST)
        return jnp.where(
            col_index > block_step,
            current - update,
            jnp.where(col_index == block_step, solved[:, None, :], current),
        )

    for block_step in range(STEPS):
        local_block = block_step // cols_axis
        first_col = block_step * block_size
        diag_block = right_rows[local_block, :, first_col : first_col + block_size]
        solved = lax.cond(
            my_col == block_step % cols_axis,
            solve_right,
            nothing_left,
            (diag_block, columns[:, local_block]),
        )
        solved = spread(solved, "pcol", block_step % cols_axis)
        columns = right_update(columns, solved, block_step)
    return columns.reshape(cross_cov.shape)


def solution(mesh):
    placed = (
        P(None, "prow", None, None, "pcol", None),
        P(None, "prow", None, "pcol"),
        P(None, "pcol", None, "prow"),
    )
    return jax.shard_map(
        shards,
        mesh=mesh,
        in_specs=placed,
        out_specs=P(None, "prow", None, None, "pcol", None),
        check_vma=False,
    )
```

profile of v0, /device:TPU:0, one launch (start us, length us, event | category | flops | bytes accessed | tf_op | source)
XLA Modules:
  0.0 603.8 jit_solution(9120524464685021274)
XLA Ops:
  7.3 27.1 %all-gather.3.cloned.1.call-done = f32[4,1,256,512]{3,2,0,1:T(8,128)} async-done(((f32[4,1,256,128]{3,2,0,1:T(8,128)}), f32[4,1,256,512]{3,2,0,1:T(8,128)}) %all-gather.3.cloned.1.call-update) | async-done | bytes 2097168 | tf_op jit(solution)/shard_map/all_gather | solution.py:36
  34.5 34.7 %conditional.4 = (f32[256,2048]{0,1:T(8,128)}) conditional(s32[]{:T(128)} %convert_element_type.12, () %tuple.31, (f32[4,256,512]{2,1,0:T(8,128)}, f32[4,1,256,8,1,256]{5,4,3,2,1,0:T(1,128)}) %tuple.153), branch_computations={%region_0.0_spmd, %region_1.0_spmd} | conditional | flops 1208877056 | bytes 41746636 | solution.py:55
  34.5 3.9 copy.30
  40.5 3.9 while.8
  44.4 19.7 %custom-call.8 = f32[2,128,128]{1,2,0:T(8,128)S(1)} custom-call(f32[2,128,128]{2,1,0:T(8,128)S(1)} %get-tuple-element.87), custom_call_target="InvertDiagBlocksLowerTriangular" | custom-call | tf_op jit(solution)/shard_map/cond/branch_1_fun/jit(_solve_triangular)/triangular_solve | solution.py:16
  69.2 3.1 broadcast_select_fusion.1
  72.5 20.6 %copy.28 = f32[4,1,256,8,1,256]{2,5,3,0,4,1:T(8,128)} copy(f32[4,1,256,8,1,256]{5,4,3,2,1,0:T(1,128)} %param.15) | data formatting | bytes 16777216 | tf_op args[0]
  93.2 77.7 %all-reduce.5.cloned.1.call-done = f32[256,2048]{0,1:T(8,128)} async-done(((f32[256,2048]{0,1:T(8,128)}), f32[256,2048]{0,1:T(8,128)}) %all-reduce.5.cloned.1.call-update) | async-done | bytes 2097168 | tf_op jit(solution)/shard_map/psum | solution.py:11
  170.9 13.9 %fusion.17 = f32[4,256,2048]{1,2,0:T(8,128)} fusion(f32[4,256,2048]{1,2,0:T(8,128)} %bitcast.129, f32[256,2048]{0,1:T(8,128)} %all-reduce.5.cloned.1.call-done, pred[4]{0:T(512)(128)(4,1)S(1)} %get-tuple-element.153, pred[4]{0:T(512)(128)(4,1)S(1)} %get-tuple-element.154, f32[4,256,512]{2,1,0:T(8,128)} %bitcast.139), kind=kOutput, calls=%fused_computation.58 | convolution fusion | flops 6448742400 | bytes 22020104 | tf_op jit(solution)/shard_map/cij,jn->cin/dot_general | solution.py:44
  189.2 139.5 %all-reduce.7.cloned.1.call-done = f32[256,2048]{0,1:T(8,128)} async-done(((f32[256,2048]{0,1:T(8,128)}), f32[256,2048]{0,1:T(8,128)}) %all-reduce.7.cloned.1.call-update) | async-done | bytes 2097168 | tf_op jit(solution)/shard_map/psum | solution.py:11
  328.7 14.2 %fusion.16 = f32[4,256,2048]{1,2,0:T(8,128)} fusion(f32[4,256,2048]{1,2,0:T(8,128)} %fusion.17, f32[256,2048]{0,1:T(8,128)} %all-reduce.7.cloned.1.call-done, pred[4]{0:T(512)(128)(4,1)S(1)} %get-tuple-element.155, pred[4]{0:T(512)(128)(4,1)S(1)} %get-tuple-element.156, f32[4,256,512]{2,1,0:T(8,128)S(1)} %bitcast.141), kind=kOutput, calls=%fused_computation.56 | convolution fusion | flops 6448742400 | bytes 22021120 | tf_op jit(solution)/shard_map/cij,jn->cin/dot_general | solution.py:44
  342.9 8.8 %copy.34 = f32[4,256,2048]{2,1,0:T(8,128)} copy(f32[4,256,2048]{1,2,0:T(8,128)} %fusion.16) | data formatting | bytes 16777216 | tf_op jit(solution)/shard_map/jit(_where)/select_n | solution.py:45
  351.7 10.9 %copy.53 = f32[128,8,8,256]{3,2,1,0:T(8,128)} copy(f32[128,8,8,256]{3,1,2,0:T(8,128)} %bitcast.130) | data formatting | bytes 16777216
  362.6 40.2 %all-gather.5.cloned.1.call-done = f32[8,1,256,512]{2,0,1,3:T(8,128)} async-done(((f32[8,1,256,64]{2,0,1,3:T(8,128)}), f32[8,1,256,512]{2,0,1,3:T(8,128)}) %all-gather.5.cloned.1.call-update) | async-done | bytes 4194320 | tf_op jit(solution)/shard_map/all_gather | solution.py:37
  402.8 5.3 copy.36
  408.1 37.0 %conditional.6 = (f32[1024,256]{1,0:T(8,128)S(1)}) conditional(s32[]{:T(128)} %convert_element_type.14, () %tuple.35, (f32[8,256,512]{2,1,0:T(8,128)}, f32[1024,8,256]{2,1,0:T(8,128)}) %tuple.151), branch_computations={%region_6.8_spmd, %region_7.10_spmd} | conditional | flops 604504064 | bytes 27590860 | solution.py:80
  408.5 8.7 %copy.37 = f32[1024,8,256]{0,2,1:T(8,128)} copy(f32[1024,8,256]{2,1,0:T(8,128)} %get-tuple-element.106) | data formatting | bytes 16777216 | tf_op jit(solution)/shard_map
  419.6 3.6 while.10
  423.2 19.7 %custom-call.10 = f32[2,128,128]{1,2,0:T(8,128)S(1)} custom-call(f32[2,128,128]{2,1,0:T(8,128)S(1)} %get-tuple-element.89), custom_call_target="InvertDiagBlocksLowerTriangular" | custom-call | tf_op jit(solution)/shard_map/cond/branch_1_fun/jit(_solve_triangular)/triangular_solve | solution.py:21
  446.3 34.0 %all-reduce.9.cloned.1.call-done = f32[1024,256]{1,0:T(8,128)} async-done(((f32[1024,256]{1,0:T(8,128)}), f32[1024,256]{1,0:T(8,128)}) %all-reduce.9.cloned.1.call-update) | async-done | bytes 1048592 | tf_op jit(solution)/shard_map/psum | solution.py:11
  480.4 17.0 %select_select_fusion.1 = f32[1024,8,256]{2,0,1:T(8,128)} fusion(f32[1024,8,256]{2,1,0:T(8,128)} %bitcast.127, f32[1024,256]{1,0:T(8,128)} %all-reduce.9.cloned.1.call-done, pred[8]{0:T(512)(128)(4,1)S(1)} %get-tuple-element.157, pred[8]{0:T(512)(128)(4,1)S(1)} %get-tuple-element.158, f32[8,256,512]{2,1,0:T(8,128)} %bitcast.132), kind=kOutput, calls=%fused_computation.60 | convolution fusion | flops 6448742400 | bytes 20971536 | tf_op jit(solution)/shard_map/rj,dsj->rds/dot_general | solution.py:69
  498.7 72.5 %all-reduce.11.cloned.1.call-done = f32[1024,256]{1,0:T(8,128)} async-done(((f32[1024,256]{1,0:T(8,128)}), f32[1024,256]{1,0:T(8,128)}) %all-reduce.11.cloned.1.call-update) | async-done | bytes 1048592 | tf_op jit(solution)/shard_map/psum | solution.py:11
  571.2 12.9 %select_select_fusion = f32[1024,8,256]{2,0,1:T(8,128)S(1)} fusion(f32[1024,8,256]{2,0,1:T(8,128)} %select_select_fusion.1, f32[1024,256]{1,0:T(8,128)} %all-reduce.11.cloned.1.call-done, pred[8]{0:T(512)(128)(4,1)S(1)} %get-tuple-element.159, pred[8]{0:T(512)(128)(4,1)S(1)} %get-tuple-element.160, f32[8,256,512]{2,1,0:T(8,128)} %bitcast.134), kind=kOutput, calls=%fused_computation.59 | convolution fusion | flops 6448742400 | bytes 20971536 | tf_op jit(solution)/shard_map/rj,dsj->rds/dot_general | solution.py:69
  584.1 12.7 %copy.43 = f32[4,1,256,8,1,256]{5,4,3,2,1,0:T(1,128)} copy(f32[4,1,256,8,1,256]{5,2,0,3,4,1:T(8,128)S(1)} %bitcast.128) | data formatting | bytes 16777216 | tf_op jit(solution)/shard_map/reshape | solution.py:88
  (61 shorter events, 28.5 us)
Async XLA Ops:
  6.5 27.9 %all-gather.3.cloned.1.call-start = ((), (), s32[]{:S(2)}) async-start(), calls=%async_computation | async-start | bytes 2621440 | tf_op jit(solution)/shard_map/all_gather | solution.py:36
  7.3 163.6 %all-reduce.5.cloned.1.call-start = ((), (), s32[]{:S(2)}) async-start(), calls=%async_computation.1 | async-start | bytes 4194304 | tf_op jit(solution)/shard_map/psum | solution.py:11
  72.3 256.5 %all-reduce.7.cloned.1.call-start = ((), (), s32[]{:S(2)}) async-start(), calls=%async_computation.2 | async-start | bytes 4194304 | tf_op jit(solution)/shard_map/psum | solution.py:11
  186.2 1.6 copy-start.1
  187.7 141.0 %copy-start = (f32[4,1,256,512]{3,2,0,1:T(8,128)S(1)}, f32[4,1,256,512]{3,2,0,1:T(8,128)}, u32[]{:S(2)}) copy-start(f32[4,1,256,512]{3,2,0,1:T(8,128)} %all-gather.3.cloned.1.call-done) | copy-start | bytes 6291460
  187.7 215.1 %all-gather.5.cloned.1.call-start = ((), (), s32[]{:S(2)}) async-start(), calls=%async_computation.3 | async-start | bytes 4718592 | tf_op jit(solution)/shard_map/all_gather | solution.py:37
  188.9 291.4 %all-reduce.9.cloned.1.call-start = ((), (), s32[]{:S(2)}) async-start(), calls=%async_computation.4 | async-start | bytes 2097152 | tf_op jit(solution)/shard_map/psum | solution.py:11
  446.3 124.9 %all-reduce.11.cloned.1.call-start = ((), (), s32[]{:S(2)}) async-start(), calls=%async_computation.5 | async-start | bytes 2097152 | tf_op jit(solution)/shard_map/psum | solution.py:11
Sparse Core Ops, SparseCore 0:
  8.9 25.5 all-gather.2
  72.4 98.4 all-reduce.4
  187.8 140.8 all-reduce.6
  330.7 72.0 all-gather.4
  446.4 33.9 all-reduce.8
  498.8 72.3 all-reduce.10
where the time goes:
time: 611 us; the launch traced here: 604 us
  waiting for transfers between devices  392 us (64%)
  local copies, waits for them, and re-layouts  85.6 us (14%)
  matrix products  62.9 us (10%)
  other arithmetic  48.3 us (8%)
  between operations  13.7 us (2%)
    psum x4, waiting for transfers between devices, spread(): return lax.psum(jnp.where(mine, x, jnp.zeros_like(x)), axis)  324 us
    all_gather x1, waiting for transfers between devices, shards(): right_rows = lax.all_gather(right_factor, 'prow', axis=3, tiled=True)[:, 0]  40.2 us
    unnamed x7, local copies, waits for them, and re-layouts  32.7 us
    dot_general x2, matrix products, right_update(): jnp.einsum('rj,dsj->rds', solved, factor, precision=lax.Precision.HIGHEST)  29.9 us
    dot_general x2, matrix products, left_update(): jnp.einsum('cij,jn->cin', factor, solved, precision=lax.Precision.HIGHEST)  28.1 us
    all_gather x1, waiting for transfers between devices, shards(): left_rows = lax.all_gather(left_factor, 'pcol', axis=3, tiled=True)[:, 0]  27.1 us
    another operation x5, other arithmetic, solve_left(): return jax.scipy.linalg.solve_triangular(diag_block, owned_rows, lower=True)  20.8 us
    another operation x4, other arithmetic, solve_right(): jax.scipy.linalg.solve_triangular(diag_block, owned_cols.T, lower=True)  20.6 us
  transfers between devices with their start and end apart: 6, of which 6 were waited for; matrix products, arithmetic and copies ran while one was open for 9% of the time, Pallas kernels for 0%

commit v1 on v0

--- a/solution.py
+++ b/solution.py
@@ -6,9 +6,13 @@
 STEPS = 2
 
 
+def refer_the_scenes(block_in, axis_key):
+    return jnp.sum(jax.lax.all_gather(block_in, axis_key), axis=0)
+
+
 def spread(x, axis, root):
     mine = lax.axis_index(axis) == root
-    return lax.psum(jnp.where(mine, x, jnp.zeros_like(x)), axis)
+    return refer_the_scenes(jnp.where(mine, x, jnp.zeros_like(x)), axis)
 
 
 def solve_left(operands):

time: 611 us -> 880 us (1.44)
  waiting for transfers between devices: 392 us -> 593 us
  matrix products: 62.9 us -> 89 us
  other arithmetic: 48.3 us -> 74.3 us
  local copies, waits for them, and re-layouts: 85.6 us -> 101 us
    all_gather x0 -> x4, waiting for transfers between devices: none -> 526 us  [refer_the_scenes(): return jnp.sum(jax.lax.all_gather(block_in, axis_key), axis=0)]
    psum x4 -> x0, waiting for transfers between devices: 324 us -> none  [spread(): return lax.psum(jnp.where(mine, x, jnp.zeros_like(x)), axis)]
    reduce_sum x0 -> x4, other arithmetic: none -> 27.7 us  [refer_the_scenes(): return jnp.sum(jax.lax.all_gather(block_in, axis_key), axis=0)]
    dot_general x2, matrix products: 28.1 us -> 41.8 us  [left_update(): jnp.einsum('cij,jn->cin', factor, solved, precision=lax.Precision.HIGHEST)]
    dot_general x2, matrix products: 29.9 us -> 42.2 us  [right_update(): jnp.einsum('rj,dsj->rds', solved, factor, precision=lax.Precision.HIGHEST)]
    all_gather x0 -> x2, local copies, waits for them, and re-layouts: none -> 12.1 us  [refer_the_scenes(): return jnp.sum(jax.lax.all_gather(block_in, axis_key), axis=0)]
    unnamed x7 -> x5, local copies, waits for them, and re-layouts: 32.7 us -> 33.8 us
  transfers between devices with their start and end apart: 6 -> 6, of which waited for: 6 -> 6; matrix products, arithmetic and copies ran while one was open for 9% -> 7% of each run, Pallas kernels for 0% -> 0%
where the time goes in v1:
time: 880 us; the launch traced here: 873 us
  waiting for transfers between devices  593 us (67%)
  local copies, waits for them, and re-layouts  101 us (11%)
  matrix products  89 us (10%)
  other arithmetic  74.3 us (8%)
  between operations  13.8 us (2%)
    all_gather x4, waiting for transfers between devices, refer_the_scenes(): return jnp.sum(jax.lax.all_gather(block_in, axis_key), axis=0)  526 us
    dot_general x2, matrix products, right_update(): jnp.einsum('rj,dsj->rds', solved, factor, precision=lax.Precision.HIGHEST)  42.2 us
    dot_general x2, matrix products, left_update(): jnp.einsum('cij,jn->cin', factor, solved, precision=lax.Precision.HIGHEST)  41.8 us
    all_gather x1, waiting for transfers between devices, shards(): right_rows = lax.all_gather(right_factor, 'prow', axis=3, tiled=True)[:, 0]  39 us
    unnamed x5, local copies, waits for them, and re-layouts  33.8 us
    reduce_sum x4, other arithmetic, refer_the_scenes(): return jnp.sum(jax.lax.all_gather(block_in, axis_key), axis=0)  27.7 us
    all_gather x1, waiting for transfers between devices, shards(): left_rows = lax.all_gather(left_factor, 'pcol', axis=3, tiled=True)[:, 0]  27.1 us
    another operation x5, other arithmetic, solve_left(): return jax.scipy.linalg.solve_triangular(diag_block, owned_rows, lower=True)  20.8 us
  transfers between devices with their start and end apart: 6, of which 6 were waited for; matrix products, arithmetic and copies ran while one was open for 7% of the time, Pallas kernels for 0%

profile of v1, /device:TPU:0, one launch (start us, length us, event | category | flops | bytes accessed | tf_op | source)
XLA Modules:
  0.0 872.5 jit_solution(8404068294229076128)
XLA Ops:
  7.3 27.1 %all-gather.11.cloned.1.call-done = f32[4,1,256,512]{3,2,0,1:T(8,128)} async-done(((f32[4,1,256,128]{3,2,0,1:T(8,128)}), f32[4,1,256,512]{3,2,0,1:T(8,128)}) %all-gather.11.cloned.1.call-update) | async-done | bytes 2097168 | tf_op jit(solution)/shard_map/all_gather | solution.py:40
  34.5 33.2 %conditional.4 = (f32[256,2048]{1,0:T(8,128)S(1)}) conditional(s32[]{:T(128)} %convert_element_type.12, () %tuple.31, (f32[4,256,512]{2,1,0:T(8,128)}, f32[4,1,256,8,1,256]{5,4,3,2,1,0:T(1,128)}) %tuple.145), branch_computations={%region_0.0_spmd, %region_1.0_spmd} | conditional | flops 1208877056 | bytes 37552324 | solution.py:59
  39.8 19.7 %custom-call.8 = f32[2,128,128]{1,2,0:T(8,128)S(1)} custom-call(f32[2,128,128]{2,1,0:T(8,128)S(1)} %get-tuple-element.87), custom_call_target="InvertDiagBlocksLowerTriangular" | custom-call | tf_op jit(solution)/shard_map/cond/branch_1_fun/jit(_solve_triangular)/triangular_solve | solution.py:20
  71.6 20.9 %copy.20 = f32[4,1,256,8,1,256]{2,5,3,0,4,1:T(8,128)} copy(f32[4,1,256,8,1,256]{5,4,3,2,1,0:T(1,128)} %param.15) | data formatting | bytes 16777216 | tf_op args[0]
  92.5 200.3 %all-gather.15.cloned.1.call-done = f32[2048,2048]{1,0:T(8,128)} async-done(((f32[256,2048]{1,0:T(8,128)}), f32[2048,2048]{1,0:T(8,128)}) %all-gather.15.cloned.1.call-update) | async-done | bytes 16777232 | tf_op jit(solution)/shard_map/all_gather | solution.py:10
  292.8 9.1 %reduce_sum.36 = f32[256,2048]{1,0:T(8,128)} reduce(f32[8,256,2048]{2,1,0:T(8,128)} %bitcast.142, f32[]{:T(128)} %constant.48.clone.1), dimensions={0}, to_apply=%region_2.4 | reduce | flops 3670016 | bytes 18874372 | tf_op jit(solution)/shard_map/reduce_sum | solution.py:10
  303.8 20.9 %fusion.17 = f32[4,256,2048]{1,2,0:T(8,128)} fusion(f32[4,256,2048]{1,2,0:T(8,128)} %bitcast.134, f32[256,2048]{0,1:T(8,128)S(1)} %copy.24, pred[4]{0:T(512)(128)(4,1)S(1)} %get-tuple-element.149, pred[4]{0:T(512)(128)(4,1)S(1)} %get-tuple-element.150, f32[256,2048]{1,0:T(8,128)} %reduce_sum.36, f32[4,256,512]{2,1,0:T(8,128)} %bitcast.147), kind=kOutput, calls=%fused_computation.58 | convolution fusion | flops 6448742400 | bytes 22020104 | tf_op jit(solution)/shard_map/cij,jn->cin/dot_general | solution.py:48
  326.9 39.0 %all-gather.13.cloned.1.call-done = f32[8,1,256,512]{2,0,1,3:T(8,128)} async-done(((f32[8,1,256,64]{2,0,1,3:T(8,128)}), f32[8,1,256,512]{2,0,1,3:T(8,128)}) %all-gather.13.cloned.1.call-update) | async-done | bytes 4194320 | tf_op jit(solution)/shard_map/all_gather | solution.py:41
  365.9 5.3 copy.30
  371.2 222.6 %all-gather.17.cloned.1.call-done = f32[2048,2048]{1,0:T(8,128)} async-done(((f32[256,2048]{1,0:T(8,128)}), f32[2048,2048]{1,0:T(8,128)}) %all-gather.17.cloned.1.call-update) | async-done | bytes 16777232 | tf_op jit(solution)/shard_map/all_gather | solution.py:10
  593.7 9.1 %reduce_sum.37 = f32[256,2048]{1,0:T(8,128)} reduce(f32[8,256,2048]{2,1,0:T(8,128)} %bitcast.141, f32[]{:T(128)} %constant.48.clone.1), dimensions={0}, to_apply=%region_5.7 | reduce | flops 3670016 | bytes 18874372 | tf_op jit(solution)/shard_map/reduce_sum | solution.py:10
  604.8 20.9 %fusion.16 = f32[4,256,2048]{1,2,0:T(8,128)} fusion(f32[4,256,2048]{1,2,0:T(8,128)} %fusion.17, f32[256,2048]{0,1:T(8,128)S(1)} %copy.27, pred[4]{0:T(512)(128)(4,1)S(1)} %get-tuple-element.151, pred[4]{0:T(512)(128)(4,1)S(1)} %get-tuple-element.152, f32[256,2048]{1,0:T(8,128)} %reduce_sum.37, f32[4,256,512]{2,1,0:T(8,128)} %bitcast.149), kind=kOutput, calls=%fused_computation.56 | convolution fusion | flops 6448742400 | bytes 22020104 | tf_op jit(solution)/shard_map/cij,jn->cin/dot_general | solution.py:48
  625.7 9.0 %copy.28 = f32[4,256,2048]{2,1,0:T(8,128)} copy(f32[4,256,2048]{1,2,0:T(8,128)} %fusion.16) | data formatting | bytes 16777216 | tf_op jit(solution)/shard_map/jit(_where)/select_n | solution.py:49
  634.6 10.9 %copy.49 = f32[128,8,8,256]{3,2,1,0:T(8,128)} copy(f32[128,8,8,256]{3,1,2,0:T(8,128)} %bitcast.136) | data formatting | bytes 16777216
  645.5 36.7 %conditional.6 = (f32[1024,256]{0,1:T(8,128)S(1)}) conditional(s32[]{:T(128)} %convert_element_type.14, () %tuple.35, (f32[8,256,512]{2,1,0:T(8,128)}, f32[1024,8,256]{2,1,0:T(8,128)}) %tuple.143), branch_computations={%region_6.8_spmd, %region_7.10_spmd} | conditional | flops 604504064 | bytes 25493700 | solution.py:84
  650.5 19.7 %custom-call.10 = f32[2,128,128]{1,2,0:T(8,128)S(1)} custom-call(f32[2,128,128]{2,1,0:T(8,128)S(1)} %get-tuple-element.89), custom_call_target="InvertDiagBlocksLowerTriangular" | custom-call | tf_op jit(solution)/shard_map/cond/branch_1_fun/jit(_solve_triangular)/triangular_solve | solution.py:25
  670.2 8.8 %copy.31 = f32[1024,8,256]{0,2,1:T(8,128)} copy(f32[1024,8,256]{2,1,0:T(8,128)} %get-tuple-element.106) | data formatting | bytes 16777216 | tf_op jit(solution)/shard_map
  683.4 31.8 %all-gather.19.cloned.1.call-done = f32[4096,256]{0,1:T(8,128)} async-done(((f32[1024,256]{0,1:T(8,128)}), f32[4096,256]{0,1:T(8,128)}) %all-gather.19.cloned.1.call-update) | async-done | bytes 4194320 | tf_op jit(solution)/shard_map/all_gather | solution.py:10
  715.2 6.1 reshape.112
  726.4 24.3 %select_select_fusion.1 = f32[1024,8,256]{2,0,1:T(8,128)} fusion(f32[1024,8,256]{2,1,0:T(8,128)} %bitcast.133, f32[1024,256]{1,0:T(8,128)S(1)} %copy.34, pred[8]{0:T(512)(128)(4,1)S(1)} %get-tuple-element.153, pred[8]{0:T(512)(128)(4,1)S(1)} %get-tuple-element.154, f32[8,256,512]{2,1,0:T(8,128)} %bitcast.138, f32[1024,256]{0,1:T(8,128)S(1)} %reduce_sum.38), kind=kOutput, calls=%fused_computation.60 | convolution fusion | flops 6448742400 | bytes 20971536 | tf_op jit(solution)/shard_map/rj,dsj->rds/dot_general | solution.py:73
  752.2 71.7 %all-gather.21.cloned.1.call-done = f32[4096,256]{0,1:T(8,128)} async-done(((f32[1024,256]{0,1:T(8,128)}), f32[4096,256]{0,1:T(8,128)}) %all-gather.21.cloned.1.call-update) | async-done | bytes 4194320 | tf_op jit(solution)/shard_map/all_gather | solution.py:10
  823.8 6.0 reshape.113
  834.9 17.9 %select_select_fusion = f32[1024,8,256]{2,0,1:T(8,128)S(1)} fusion(f32[1024,8,256]{2,0,1:T(8,128)} %select_select_fusion.1, f32[1024,256]{1,0:T(8,128)S(1)} %copy.38, pred[8]{0:T(512)(128)(4,1)S(1)} %get-tuple-element.155, pred[8]{0:T(512)(128)(4,1)S(1)} %get-tuple-element.156, f32[8,256,512]{2,1,0:T(8,128)} %bitcast.140, f32[1024,256]{0,1:T(8,128)S(1)} %reduce_sum.39), kind=kOutput, calls=%fused_computation.59 | convolution fusion | flops 6448742400 | bytes 20971536 | tf_op jit(solution)/shard_map/rj,dsj->rds/dot_general | solution.py:73
  852.8 12.7 %copy.39 = f32[4,1,256,8,1,256]{5,4,3,2,1,0:T(1,128)} copy(f32[4,1,256,8,1,256]{5,2,0,3,4,1:T(8,128)S(1)} %bitcast.135) | data formatting | bytes 16777216 | tf_op jit(solution)/shard_map/reshape | solution.py:92
  (67 shorter events, 53.5 us)
Async XLA Ops:
  6.5 27.9 %all-gather.11.cloned.1.call-start = ((), (), s32[]{:S(2)}) async-start(), calls=%async_computation | async-start | bytes 2621440 | tf_op jit(solution)/shard_map/all_gather | solution.py:40
  7.3 285.5 %all-gather.15.cloned.1.call-start = ((), (), s32[]{:S(2)}) async-start(), calls=%async_computation.2 | async-start | bytes 18874368 | tf_op jit(solution)/shard_map/all_gather | solution.py:10
  69.2 1.0 copy-start
  69.2 296.7 %all-gather.13.cloned.1.call-start = ((), (), s32[]{:S(2)}) async-start(), calls=%async_computation.1 | async-start | bytes 4718592 | tf_op jit(solution)/shard_map/all_gather | solution.py:41
  71.4 522.4 %all-gather.17.cloned.1.call-start = ((), (), s32[]{:S(2)}) async-start(), calls=%async_computation.3 | async-start | bytes 18874368 | tf_op jit(solution)/shard_map/all_gather | solution.py:10
  326.9 388.4 %all-gather.19.cloned.1.call-start = ((), (), s32[]{:S(2)}) async-start(), calls=%async_computation.4 | async-start | bytes 5242880 | tf_op jit(solution)/shard_map/all_gather | solution.py:10
  683.4 140.5 %all-gather.21.cloned.1.call-start = ((), (), s32[]{:S(2)}) async-start(), calls=%async_computation.5 | async-start | bytes 5242880 | tf_op jit(solution)/shard_map/all_gather | solution.py:10
Sparse Core Ops, SparseCore 0:
  8.9 25.5 all-gather.10
  69.3 223.3 all-gather.14
  294.9 70.9 all-gather.12
  367.9 225.7 all-gather.16
  683.5 31.7 all-gather.18
  752.3 71.5 all-gather.20
